TPU v7x, 32 devices: a whole 2x2x4 slice. The times are simulated.
32 devices in a mesh: src: 4 (over y, x), blk: 8 (over z, core).
Axes of the slice: x: 2, y: 2, z: 4, core: 2. Of those that a mesh axis runs over, the one named last changes fastest.
Arguments:
- values: float32 [4, 512, 32, 128], P('src', 'blk'), may hold values from -0.25 to 0.25
- diagonal: float32 [4, 512, 128], P('src', 'blk'), may hold values from 0.55 to 0.95
- rhs_parts: float32 [4, 512, 128], P('src', 'blk'), may hold values from -24 to 24
- owner_map: int32 [512, 128], P('blk'), may hold values from 0 to 3
- columns: int32 [512, 32, 128], P('blk'), may hold values from 0 to 1073741823
- destination: int32 [512, 1], P('blk'), may hold values from 0 to 7; in each aligned block of 64 rows (0 to 63, 64 to 127, ...) at most 16 rows name the same one
- order_keys: int32 [512], P('blk'), may hold values from 0 to 511, each once
Outputs:
- solution: float32 [512, 128], P('blk')
Inputs may be any that keep to these rules, and one draw needn't show every extreme that they name: `destination`: among the row blocks of one index of blk no owner is named more than 16 times, some owner is named exactly 16 times, and every owner is named by some block. `order_keys`: each key appears once.
All inputs are finite; a program needn't handle non-finite values.
Results may differ from a plain program's by a relative error of at most 0.0003.
Values sent between devices are 32-bit elements; how exact they have to be, the bound alone decides.
A program may use at most 64 MiB of HBM per device.

v0:
```python
import functools
import jax
import jax.numpy as jnp
from jax import lax
from jax.experimental import pallas as pl
from jax.experimental.pallas import tpu as pltpu
from jax.sharding import PartitionSpec as P

SWEEPS = 3
FAR = 3.0e38
CHUNKS = 4
CUTS = (1, 3)


def kernel(n_src, n_blk, values_hbm, columns_hbm, diag_hbm, rhs_hbm, map_hbm, dest_hbm, keys_hbm, out_ref,
           vals, mat_in, cols, diag_ref, rhs_ref, map_ref, dest_ref, keys_ref,
           comb_all, comb_sum, diag_in, rhs_in, zed, picked, nxt, prod, fin,
           load_sem, comb_send, comb_recv, dr_send, dr_recv, out_send, out_recv, zed_send, zed_recv,
           nxt_send, nxt_recv, mat_send, mat_recv):
    s = lax.axis_index("src")
    b = lax.axis_index("blk")
    tiles, rows = diag_ref.shape
    stored = vals.shape[1]
    q = tiles // n_src
    lanes = n_blk * q
    total = n_blk * tiles
    chunk = q // CHUNKS
    src_peers = [lax.rem(s + o, n_src) for o in range(1, n_src)]
    blk_peers = [lax.rem(b + o, n_blk) for o in range(1, n_blk)]
    mesh_id = pl.DeviceIdType.MESH
    started = []

    def rows_of(part):
        return pl.ds(pl.multiple_of(part * q, q), q)

    mine = rows_of(s)
    barrier = pltpu.get_barrier_semaphore()
    for peer in src_peers:
        pl.semaphore_signal(barrier, inc=1, device_id={"src": peer}, device_id_type=mesh_id)
    for peer in blk_peers:
        pl.semaphore_signal(barrier, inc=1, device_id={"blk": peer}, device_id_type=mesh_id)
    pairs = [(dest_hbm, dest_ref), (keys_hbm, keys_ref), (diag_hbm, diag_ref), (rhs_hbm, rhs_ref), (map_hbm, map_ref),
             (columns_hbm.at[mine], cols), (values_hbm.at[mine], vals)]
    loads = [pltpu.make_async_copy(src, dst, load_sem.at[i]) for i, (src, dst) in enumerate(pairs)]
    for load in loads:
        load.start()
    for load in loads[:2]:
        load.wait()

    dest_row = dest_ref[...].astype(jnp.float32)
    comb_row = dest_row * total + keys_ref[...].astype(jnp.float32) + 1.0
    eye = lax.broadcasted_iota(jnp.int32, (tiles, tiles), 0) == lax.broadcasted_iota(jnp.int32, (tiles, tiles), 1)
    comb_col = jnp.sum(jnp.where(eye, comb_row, 0.0), axis=1, keepdims=True)
    low_col = jnp.sum(jnp.where(eye, dest_row, 0.0), axis=1, keepdims=True) * total + 1.0
    at_lane = lax.broadcasted_iota(jnp.int32, (q, lanes), 1) - b * q == lax.broadcasted_iota(jnp.int32, (q, lanes), 0)
    for part in range(n_src):
        spread = jnp.where(at_lane, comb_col[part * q:(part + 1) * q], 0.0)
        comb_all[b, part:part + 1, :] = jnp.sum(spread, axis=0, keepdims=True)
    for load in loads[2:5]:
        load.wait()

    pl.semaphore_wait(barrier, n_src + n_blk - 2)

    def send(src, dst, send_sem, recv_sem, device):
        copy = pltpu.make_async_remote_copy(src_ref=src, dst_ref=dst, send_sem=send_sem, recv_sem=recv_sem,
                                            device_id=device, device_id_type=mesh_id)
        copy.start()
        started.append(copy)

    def arrive(dst, send_sem, recv_sem, device):
        pltpu.make_async_remote_copy(src_ref=dst, dst_ref=dst, send_sem=send_sem, recv_sem=recv_sem,
                                     device_id=device, device_id_type=mesh_id).wait_recv()

    def send_matrix(low, high):
        for piece in range(low, high):
            for peer in src_peers:
                there = pl.ds(pl.multiple_of(peer * q + piece * chunk, chunk), chunk)
                here = pl.ds(piece * chunk, chunk)
                send(values_hbm.at[there], mat_in.at[s, here], mat_send.at[piece, peer], mat_recv.at[piece, s], {"src": peer})

    for peer in src_peers:
        send(diag_ref.at[rows_of(peer)], diag_in.at[s], dr_send.at[0, peer], dr_recv.at[0, s], {"src": peer})
        send(rhs_ref.at[rows_of(peer)], rhs_in.at[s], dr_send.at[1, peer], dr_recv.at[1, s], {"src": peer})
    for peer in blk_peers:
        send(comb_all.at[b], comb_all.at[b], comb_send.at[peer], comb_recv.at[b], {"blk": peer})
    send_matrix(0, CUTS[0])

    diag_q = diag_ref[mine, :]
    owner_q = map_ref[mine, :]
    right_q = jnp.where(owner_q == s, rhs_ref[mine, :], 0.0)
    for peer in src_peers:
        arrive(diag_in.at[peer], dr_send.at[0, peer], dr_recv.at[0, peer], {"src": peer})
        diag_q = diag_q + diag_in[peer]
        arrive(rhs_in.at[peer], dr_send.at[1, peer], dr_recv.at[1, peer], {"src": peer})
        right_q = jnp.where(owner_q == peer, rhs_in[peer], right_q)

    def share(step, x_q):
        zed[step, b] = x_q
        for peer in blk_peers:
            send(zed.at[step, b], zed.at[step, b], zed_send.at[step, peer], zed_recv.at[step, b], {"blk": peer})

    def product(step):
        def block(t, carry):
            code = cols[t]
            if step == 0:
                entry = vals[t]
                for peer in src_peers:
                    entry = entry + mat_in[peer, t]
                vals[t] = entry
            else:
                entry = vals[t]
            lane = code & (rows - 1)
            x = jnp.broadcast_to(zed[step, b, pl.ds(t, 1), :], (stored, rows))
            y = jnp.broadcast_to(nxt[step, s, pl.ds(t, 1), :], (stored, rows))
            near = jnp.take_along_axis(x, lane, axis=1, mode="promise_in_bounds")
            far = jnp.take_along_axis(y, lane, axis=1, mode="promise_in_bounds")
            term = jnp.where((code & rows) != 0, far, near) * entry
            prod[pl.ds(t, 1), :] = jnp.sum(term, axis=0, keepdims=True)
            return carry

        lax.fori_loop(0, q, block, 0, unroll=8)
        return prod[...]

    share(0, right_q / diag_q)
    send_matrix(CUTS[0], CUTS[1])

    for peer in blk_peers:
        arrive(comb_all.at[peer], comb_send.at[peer], comb_recv.at[peer], {"blk": peer})
    all_combs = comb_all[0]
    for other in range(1, n_blk):
        all_combs = all_combs + comb_all[other]
    comb_sum[...] = all_combs
    after = jnp.full((tiles, 1), FAR, jnp.float32)
    least = jnp.full((tiles, 1), FAR, jnp.float32)
    for part in range(n_src):
        line = comb_sum[part:part + 1, :]
        later = (line > comb_col) & (line < low_col + total)
        after = jnp.minimum(after, jnp.min(jnp.where(later, line, FAR), axis=1, keepdims=True))
        least = jnp.minimum(least, jnp.min(jnp.where(line >= low_col, line, FAR), axis=1, keepdims=True))
    follow = jnp.where(after < FAR, after, least)
    choice = jnp.where(comb_sum[pl.ds(s, 1), :] == follow, 1.0, 0.0).astype(jnp.bfloat16)

    for step in range(SWEEPS - 1):
        for peer in blk_peers:
            arrive(zed.at[step, peer], zed_send.at[step, peer], zed_recv.at[step, peer], {"blk": peer})
        spread = zed[step].reshape(lanes, rows)
        high = spread.astype(jnp.bfloat16)
        rest = spread - high.astype(jnp.float32)
        middle = rest.astype(jnp.bfloat16)
        small = (rest - middle.astype(jnp.float32)).astype(jnp.bfloat16)
        got = jnp.dot(choice, high, preferred_element_type=jnp.float32)
        got = got + jnp.dot(choice, middle, preferred_element_type=jnp.float32)
        got = got + jnp.dot(choice, small, preferred_element_type=jnp.float32)
        picked[step] = got
        for peer in src_peers:
            send(picked.at[step, rows_of(peer)], nxt.at[step, s], nxt_send.at[step, peer], nxt_recv.at[step, s], {"src": peer})
        if step == 0:
            send_matrix(CUTS[1], CHUNKS)
            for load in loads[5:]:
                load.wait()
        ahead = picked[step, mine, :]
        for peer in src_peers:
            arrive(nxt.at[step, peer], nxt_send.at[step, peer], nxt_recv.at[step, peer], {"src": peer})
            ahead = ahead + nxt[step, peer]
        nxt[step, s] = ahead
        if step == 0:
            for piece in range(CHUNKS):
                for peer in src_peers:
                    here = pl.ds(piece * chunk, chunk)
                    arrive(mat_in.at[peer, here], mat_send.at[piece, peer], mat_recv.at[piece, peer], {"src": peer})
        x_q = (right_q - product(step)) / diag_q
        if step < SWEEPS - 2:
            share(step + 1, x_q)
    fin[mine, :] = x_q
    for peer in src_peers:
        send(fin.at[mine], fin.at[mine], out_send.at[peer], out_recv.at[s], {"src": peer})
    for peer in src_peers:
        arrive(fin.at[rows_of(peer)], out_send.at[peer], out_recv.at[peer], {"src": peer})
    out_ref[...] = fin[...]
    for copy in started:
        copy.wait_send()


def on_device(values, diagonal, rhs_parts, owner_map, columns, destination, order_keys):
    n_src = lax.axis_size("src")
    n_blk = lax.axis_size("blk")
    tiles, rows = diagonal.shape[1:]
    stored = values.shape[2]
    q = tiles // n_src
    f32 = jnp.float32
    i32 = jnp.int32
    dma = pltpu.SemaphoreType.DMA
    later = SWEEPS - 1
    return pl.pallas_call(
        functools.partial(kernel, n_src, n_blk),
        out_shape=pltpu.VMEM((tiles, rows), f32),
        in_specs=[pl.BlockSpec(memory_space=pl.ANY)] * 7,
        out_specs=pl.BlockSpec(memory_space=pltpu.VMEM),
        scratch_shapes=[
            pltpu.VMEM((q, stored, rows), f32),
            pltpu.VMEM((n_src, q, stored, rows), f32),
            pltpu.VMEM((q, stored, rows), i32),
            pltpu.VMEM((tiles, rows), f32),
            pltpu.VMEM((tiles, rows), f32),
            pltpu.VMEM((tiles, rows), i32),
            pltpu.VMEM((1, tiles), i32),
            pltpu.VMEM((1, tiles), i32),
            pltpu.VMEM((n_blk, n_src, n_blk * q), f32),
            pltpu.VMEM((n_src, n_blk * q), f32),
            pltpu.VMEM((n_src, q, rows), f32),
            pltpu.VMEM((n_src, q, rows), f32),
            pltpu.VMEM((later, n_blk, q, rows), f32),
            pltpu.VMEM((later, tiles, rows), f32),
            pltpu.VMEM((later, n_src, q, rows), f32),
            pltpu.VMEM((q, rows), f32),
            pltpu.VMEM((tiles, rows), f32),
            dma((7,)),
            dma((n_blk,)), dma((n_blk,)),
            dma((2, n_src)), dma((2, n_src)),
            dma((n_src,)), dma((n_src,)),
            dma((later, n_blk)), dma((later, n_blk)),
            dma((later, n_src)), dma((later, n_src)),
            dma((CHUNKS, n_src)), dma((CHUNKS, n_src)),
        ],
        compiler_params=pltpu.CompilerParams(collective_id=0, has_side_effects=True),
    )(values[0], columns, diagonal[0], rhs_parts[0], owner_map, destination.reshape(1, tiles), order_keys.reshape(1, tiles))


def solution(mesh):
    placed = (
        P("src", "blk", None, None),
        P("src", "blk", None),
        P("src", "blk", None),
        P("blk", None),
        P("blk", None, None),
        P("blk", None),
        P("blk"),
    )
    return jax.shard_map(
        on_device, mesh=mesh, in_specs=placed, out_specs=P("blk", None), check_vma=False
    )
```

profile of v0, /device:TPU:0, one launch (start us, length us, event | category | flops | bytes accessed | tf_op | source)
XLA Modules:
  0.0 31.8 jit_solution(13571674444710549409)
XLA Ops:
  0.0 31.2 %shard_map.73 = f32[64,128]{1,0:T(8,128)S(1)} custom-call(f32[64,32,128]{2,1,0:T(8,128)} %bitcast.5, s32[64,32,128]{2,1,0:T(8,128)} %columns_hbm.1, f32[64,128]{1,0:T(8,128)} %bitcast.6, f32[64,128]{1,0:T(8,128)} %bitcast.7, s32[64,128]{1,0:T(8,128)} %map_hbm.1, s32[1,64]{1,0:T(1,128)} %bitcast.8, s32[1,64]{1,0:T(1,128)} %bitcast.9), custom_call_target="tpu_custom_call" | custom-call | tf_op jit(solution)/shard_map/pallas_call | solution.py:194
  31.2 0.6 %copy.9 = f32[64,128]{1,0:T(8,128)} copy(f32[64,128]{1,0:T(8,128)S(1)} %shard_map.73) | data formatting | bytes 65536
where the time goes:
time: 32 us; the launch traced here: 31.8 us
  Pallas kernels  31.2 us (98%)
  local copies, waits for them, and re-layouts  0.62 us (2%)
    pallas_call x1, Pallas kernels, on_device(): pl.pallas_call(functools.partial(kernel, n_src, n_blk), out_shape=pltpu.V...  31.2 us

commit v1 on v0

v1 whole, which is shorter than its diff:
```python
import functools
import jax
import jax.numpy as jnp
from jax import lax
from jax.experimental import pallas as pl
from jax.experimental.pallas import tpu as pltpu
from jax.sharding import PartitionSpec as P

SWEEPS = 3
PIECES = 2
HALVES = 2


def kernel(n_src, n_blk, values_hbm, columns_hbm, diag_hbm, rhs_hbm, map_hbm, dest_hbm, keys_hbm, out_ref,
           vals, mat_in, cols, dr, map_ref, dest_ref, keys_ref, comb_all, comb_sum,
           iterate, snd, rcv, far, acc, psnd, prcv, total_ref,
           load_sem, comb_send, comb_recv, dr_send, dr_recv, mat_send, mat_recv,
           zed_send, zed_recv, p_send, p_recv):
    s = lax.axis_index("src")
    b = lax.axis_index("blk")
    tiles, rows = map_ref.shape
    stored = vals.shape[1]
    q = tiles // n_src
    lanes = n_blk * q
    total = n_blk * tiles
    piece_q = q // PIECES
    top = n_src // 2
    low_bit = lax.rem(s, 2)
    high_bit = s // top
    near_peer = s + 1 - 2 * low_bit
    side_peer = s + top - 2 * top * high_bit
    both_peer = near_peer + top - 2 * top * high_bit
    src_peers = [near_peer, side_peer, both_peer]
    blk_peers = [lax.rem(b + o, n_blk) for o in range(1, n_blk)]
    mesh_id = pl.DeviceIdType.MESH
    started = []
    mine = [low_bit, top + high_bit]
    other = [1 - low_bit, top + 1 - high_bit]
    partner = [near_peer, side_peer]

    def quarter(part, low=0, size=q):
        return pl.ds(pl.multiple_of(part * q + low, size), size)

    barrier = pltpu.get_barrier_semaphore()
    for peer in src_peers:
        pl.semaphore_signal(barrier, inc=1, device_id={"src": peer}, device_id_type=mesh_id)
    for peer in blk_peers:
        pl.semaphore_signal(barrier, inc=1, device_id={"blk": peer}, device_id_type=mesh_id)
    pairs = [(dest_hbm, dest_ref), (keys_hbm, keys_ref), (diag_hbm, dr.at[s, 0]), (rhs_hbm, dr.at[s, 1]), (map_hbm, map_ref),
             (values_hbm, vals)]
    pairs += [(columns_hbm.at[quarter(mine[h])], cols.at[h]) for h in range(HALVES)]
    loads = [pltpu.make_async_copy(src, dst, load_sem.at[i]) for i, (src, dst) in enumerate(pairs)]
    for load in loads:
        load.start()
    for load in loads[:2]:
        load.wait()

    dest_row = dest_ref[...].astype(jnp.float32)
    comb_row = dest_row * total + keys_ref[...].astype(jnp.float32) + 1.0
    eye = lax.broadcasted_iota(jnp.int32, (tiles, tiles), 0) == lax.broadcasted_iota(jnp.int32, (tiles, tiles), 1)
    comb_col = jnp.sum(jnp.where(eye, comb_row, 0.0), axis=1, keepdims=True)
    low_col = jnp.sum(jnp.where(eye, dest_row, 0.0), axis=1, keepdims=True) * total + 1.0
    at_lane = lax.broadcasted_iota(jnp.int32, (q, lanes), 1) - b * q == lax.broadcasted_iota(jnp.int32, (q, lanes), 0)
    for part in range(n_src):
        spread = jnp.where(at_lane, comb_col[part * q:(part + 1) * q], 0.0)
        comb_all[b, part:part + 1, :] = jnp.sum(spread, axis=0, keepdims=True)
    for load in loads[2:6]:
        load.wait()

    pl.semaphore_wait(barrier, n_src + n_blk - 2)

    def send(src, dst, send_sem, recv_sem, device):
        copy = pltpu.make_async_remote_copy(src_ref=src, dst_ref=dst, send_sem=send_sem, recv_sem=recv_sem,
                                            device_id=device, device_id_type=mesh_id)
        copy.start()
        started.append(copy)

    def arrive(dst, send_sem, recv_sem, device):
        pltpu.make_async_remote_copy(src_ref=dst, dst_ref=dst, send_sem=send_sem, recv_sem=recv_sem,
                                     device_id=device, device_id_type=mesh_id).wait_recv()

    for peer in blk_peers:
        send(comb_all.at[b], comb_all.at[b], comb_send.at[peer], comb_recv.at[b], {"blk": peer})
    for peer in src_peers:
        send(dr.at[s], dr.at[s], dr_send.at[peer], dr_recv.at[s], {"src": peer})
    for piece in range(PIECES):
        for h in range(HALVES):
            there = quarter(other[h], piece * piece_q, piece_q)
            here = pl.ds(piece * piece_q, piece_q)
            send(vals.at[there], mat_in.at[h, here], mat_send.at[h, piece], mat_recv.at[h, piece], {"src": partner[h]})

    for peer in blk_peers:
        arrive(comb_all.at[peer], comb_send.at[peer], comb_recv.at[peer], {"blk": peer})
    all_combs = comb_all[0]
    for one in range(1, n_blk):
        all_combs = all_combs + comb_all[one]
    comb_sum[...] = all_combs
    before = jnp.zeros((tiles, lanes), jnp.float32)
    last = jnp.zeros((tiles, lanes), jnp.float32)
    for part in range(n_src):
        line = comb_sum[part:part + 1, :]
        owned = jnp.where((line >= low_col) & (line < low_col + total), line, 0.0)
        before = jnp.maximum(before, jnp.where(owned < comb_col, owned, 0.0))
        last = jnp.maximum(last, owned)
    before = jnp.max(before, axis=1, keepdims=True)
    last = jnp.max(last, axis=1, keepdims=True)
    previous = jnp.where(before > 0.0, before, last)
    choices = []
    for h in range(HALVES):
        chosen = jnp.where(comb_sum[pl.ds(mine[h], 1), :] == previous, 1.0, 0.0)
        choices.append(jnp.concatenate([chosen] * 3, axis=0).T.astype(jnp.bfloat16))

    def share(step, x):
        iterate[...] = x
        high = x.astype(jnp.bfloat16)
        rest = x - high.astype(jnp.float32)
        middle = rest.astype(jnp.bfloat16)
        small = (rest - middle.astype(jnp.float32)).astype(jnp.bfloat16)
        parts = jnp.concatenate([high, middle, small], axis=0)
        for h in range(HALVES):
            got = jnp.dot(choices[h], parts, preferred_element_type=jnp.float32)
            snd[step, :, h] = got.reshape(n_blk, q, rows)
        for peer in blk_peers:
            send(snd.at[step, peer], rcv.at[step, b], zed_send.at[step, peer], zed_recv.at[step, b], {"blk": peer})

    def product(h, low, size, vector, start, take_far, first):
        def block(i, carry):
            t = low + i
            code = cols[h, t]
            entry = vals[mine[h] * q + t]
            if first:
                entry = entry + mat_in[h, t]
                vals[mine[h] * q + t] = entry
            x = jnp.broadcast_to(vector[pl.ds(start + t, 1), :], (stored, rows))
            got = jnp.take_along_axis(x, code & (rows - 1), axis=1, mode="promise_in_bounds")
            wanted = (code & rows) != 0 if take_far else (code & rows) == 0
            term = jnp.where(wanted, got * entry, 0.0)
            slim = jnp.sum(term.reshape(stored // 8, 8, rows), axis=0)
            acc[h, t] = acc[h, t] + slim if take_far else slim
            return carry

        lax.fori_loop(0, size, block, 0, unroll=8)

    for peer in src_peers:
        arrive(dr.at[peer], dr_send.at[peer], dr_recv.at[peer], {"src": peer})
    diag = dr[0, 0]
    for one in range(1, n_src):
        diag = diag + dr[one, 0]
    owner = map_ref[...]
    right = jnp.where(owner == 0, dr[0, 1], 0.0)
    for one in range(1, n_src):
        right = jnp.where(owner == one, dr[one, 1], right)

    share(0, right / diag)
    for load in loads[6:]:
        load.wait()

    for step in range(SWEEPS - 1):
        for piece in range(PIECES):
            for h in range(HALVES):
                here = pl.ds(piece * piece_q, piece_q)
                if step == 0:
                    arrive(mat_in.at[h, here], mat_send.at[h, piece], mat_recv.at[h, piece], {"src": partner[h]})
                product(h, piece * piece_q, piece_q, iterate, mine[h] * q, False, step == 0)
        for peer in blk_peers:
            arrive(rcv.at[step, peer], zed_send.at[step, peer], zed_recv.at[step, peer], {"blk": peer})
        ahead = snd[step, b]
        for peer in blk_peers:
            ahead = ahead + rcv[step, peer]
        far[...] = ahead.reshape(HALVES * q, rows)
        for h in range(HALVES):
            product(h, 0, q, far, h * q, True, False)
        psnd[step] = jnp.sum(acc[...], axis=2)
        for peer in src_peers:
            send(psnd.at[step], prcv.at[step, s], p_send.at[step, peer], p_recv.at[step, s], {"src": peer})
        for peer in src_peers:
            arrive(prcv.at[step, peer], p_send.at[step, peer], p_recv.at[step, peer], {"src": peer})
        total_ref[quarter(mine[0]), :] = psnd[step, 0] + prcv[step, side_peer, 0]
        total_ref[quarter(mine[1]), :] = psnd[step, 1] + prcv[step, near_peer, 1]
        total_ref[quarter(other[0]), :] = prcv[step, near_peer, 0] + prcv[step, both_peer, 0]
        total_ref[quarter(other[1]), :] = prcv[step, side_peer, 1] + prcv[step, both_peer, 1]
        x = (right - total_ref[...]) / diag
        if step < SWEEPS - 2:
            share(step + 1, x)
    out_ref[...] = x
    for copy in started:
        copy.wait_send()


def on_device(values, diagonal, rhs_parts, owner_map, columns, destination, order_keys):
    n_src = lax.axis_size("src")
    n_blk = lax.axis_size("blk")
    tiles, rows = diagonal.shape[1:]
    stored = values.shape[2]
    q = tiles // n_src
    f32 = jnp.float32
    i32 = jnp.int32
    dma = pltpu.SemaphoreType.DMA
    later = SWEEPS - 1
    return pl.pallas_call(
        functools.partial(kernel, n_src, n_blk),
        out_shape=pltpu.VMEM((tiles, rows), f32),
        in_specs=[pl.BlockSpec(memory_space=pl.ANY)] * 7,
        out_specs=pl.BlockSpec(memory_space=pltpu.VMEM),
        scratch_shapes=[
            pltpu.VMEM((tiles, stored, rows), f32),
            pltpu.VMEM((HALVES, q, stored, rows), f32),
            pltpu.VMEM((HALVES, q, stored, rows), i32),
            pltpu.VMEM((n_src, 2, tiles, rows), f32),
            pltpu.VMEM((tiles, rows), i32),
            pltpu.VMEM((1, tiles), i32),
            pltpu.VMEM((1, tiles), i32),
            pltpu.VMEM((n_blk, n_src, n_blk * q), f32),
            pltpu.VMEM((n_src, n_blk * q), f32),
            pltpu.VMEM((tiles, rows), f32),
            pltpu.VMEM((later, n_blk, HALVES, q, rows), f32),
            pltpu.VMEM((later, n_blk, HALVES, q, rows), f32),
            pltpu.VMEM((HALVES * q, rows), f32),
            pltpu.VMEM((HALVES, q, 8, rows), f32),
            pltpu.VMEM((later, HALVES, q, rows), f32),
            pltpu.VMEM((later, n_src, HALVES, q, rows), f32),
            pltpu.VMEM((tiles, rows), f32),
            dma((8,)),
            dma((n_blk,)), dma((n_blk,)),
            dma((n_src,)), dma((n_src,)),
            dma((HALVES, PIECES)), dma((HALVES, PIECES)),
            dma((later, n_blk)), dma((later, n_blk)),
            dma((later, n_src)), dma((later, n_src)),
        ],
        compiler_params=pltpu.CompilerParams(collective_id=0, has_side_effects=True),
    )(values[0], columns, diagonal[0], rhs_parts[0], owner_map, destination.reshape(1, tiles), order_keys.reshape(1, tiles))


def solution(mesh):
    placed = (
        P("src", "blk", None, None),
        P("src", "blk", None),
        P("src", "blk", None),
        P("blk", None),
        P("blk", None, None),
        P("blk", None),
        P("blk"),
    )
    return jax.shard_map(
        on_device, mesh=mesh, in_specs=placed, out_specs=P("blk", None), check_vma=False
    )
```

time: 32 us -> 29.9 us (0.934)
  Pallas kernels: 31.2 us -> 29.2 us
    pallas_call x1, Pallas kernels: 31.2 us -> 29.2 us  [on_device(): pl.pallas_call(functools.partial(kernel, n_src, n_blk), out_shape=pltpu.V...]
where the time goes in v1:
time: 29.9 us; the launch traced here: 29.8 us
  Pallas kernels  29.2 us (98%)
  local copies, waits for them, and re-layouts  0.62 us (2%)
    pallas_call x1, Pallas kernels, on_device(): pl.pallas_call(functools.partial(kernel, n_src, n_blk), out_shape=pltpu.V...  29.2 us
    unnamed x1, local copies, waits for them, and re-layouts  0.62 us

profile of v1, /device:TPU:0, one launch (start us, length us, event | category | flops | bytes accessed | tf_op | source)
XLA Modules:
  0.0 29.8 jit_solution(14179537151919252444)
XLA Ops:
  0.0 29.2 %shard_map.73 = f32[64,128]{1,0:T(8,128)S(1)} custom-call(f32[64,32,128]{2,1,0:T(8,128)} %bitcast.5, s32[64,32,128]{2,1,0:T(8,128)} %columns_hbm.1, f32[64,128]{1,0:T(8,128)} %bitcast.6, f32[64,128]{1,0:T(8,128)} %bitcast.7, s32[64,128]{1,0:T(8,128)} %map_hbm.1, s32[1,64]{1,0:T(1,128)} %bitcast.8, s32[1,64]{1,0:T(1,128)} %bitcast.9), custom_call_target="tpu_custom_call" | custom-call | tf_op jit(solution)/shard_map/pallas_call | solution.py:200
  29.2 0.6 %copy.9 = f32[64,128]{1,0:T(8,128)} copy(f32[64,128]{1,0:T(8,128)S(1)} %shard_map.73) | data formatting | bytes 65536
